TPU v7x, 32 devices: a whole 2x2x4 slice. The times are simulated.
32 devices in a mesh: gx: 4 (over y, x), gy: 4 (over z), gz: 2 (over core).
Axes of the slice: x: 2, y: 2, z: 4, core: 2. Of those that a mesh axis runs over, the one named last changes fastest.
Arguments:
- blocks: int32 [32768, 4], P(('gx', 'gy', 'gz')), may hold values from 0 to 15, as said below
- coefficients: bfloat16 [32768, 4, 128], P(('gx', 'gy', 'gz')), may hold values from -80 to 80
- residuals: float32 [32768], P(('gx', 'gy', 'gz')), may hold values from -3000 to 3000
Outputs:
- factor: float32 [4, 4, 128, 4, 4, 128], P('gx', None, None, 'gy')
- solution: float32 [16, 128], replicated
Inputs may be any that keep to these rules, and one draw needn't show every extreme that they name: Each row names 4 different blocks.
All inputs are finite; a program needn't handle non-finite values.
Results may differ from a plain program's by a relative error of at most 0.0003.
Values sent between devices are 32-bit elements; how exact they have to be, the bound alone decides.
A program may use at most 128 MiB of HBM per device.

v0:
```python
import jax
import jax.numpy as jnp
from jax import lax
from jax.sharding import PartitionSpec as P

G = 2048
BS = 128


def from_root(block, axis, source):
    block = jnp.where(lax.axis_index(axis) == source, block, jnp.zeros_like(block))
    return lax.psum(block, axis)


def on_device(blocks, coefficients, residuals):
    row_count = lax.axis_size("gx")
    col_count = lax.axis_size("gy")
    row_index = lax.axis_index("gx")
    col_index = lax.axis_index("gy")
    scale = 1.0 / (coefficients.shape[0] * row_count * col_count * lax.axis_size("gz"))
    width = coefficients.shape[2]
    nblock = G // BS
    per_dev = nblock // row_count
    target = (
        jnp.arange(per_dev, dtype=jnp.int32)[None, :] * row_count
        + jnp.arange(row_count, dtype=jnp.int32)[:, None]
    ).reshape(-1)
    placed = (blocks[:, :, None] == target[None, None, :]).astype(jnp.bfloat16)
    design = jnp.einsum("osz,osx->ozx", placed, coefficients, preferred_element_type=jnp.float32)
    design = design.astype(jnp.bfloat16).reshape(-1, row_count, per_dev, width)
    natural = (blocks[:, :, None] == jnp.arange(nblock, dtype=jnp.int32)[None, None, :]).astype(
        jnp.float32
    )
    weighted = coefficients.astype(jnp.float32) * residuals[:, None, None]
    rhs_local = (
        jnp.einsum("osb,osx->bx", natural, weighted, precision=lax.Precision.HIGHEST) * scale
    )
    rhs = lax.psum(rhs_local, ("gx", "gy", "gz"))
    term = (
        jnp.einsum("opix,oqjy->pqixjy", design, design, preferred_element_type=jnp.float32) * scale
    )
    term = term.reshape(row_count * col_count, per_dev, width, per_dev, width)
    halves = lax.psum_scatter(term, "gz", scatter_dimension=2, tiled=True)
    halves = lax.psum_scatter(halves, ("gx", "gy"), scatter_dimension=0, tiled=True)
    summed = lax.all_gather(halves, "gz", axis=2, tiled=True)
    matrix = summed.reshape(per_dev, width, per_dev, width)
    zero = jnp.zeros((), jnp.int32)
    block_ids = (
        jnp.arange(per_dev, dtype=jnp.int32)[None, :] * row_count
        + jnp.arange(row_count, dtype=jnp.int32)[:, None]
    )

    def factor_step(step, state):
        working, factor, pivots = state
        step_row = step % row_count
        step_local_row = step // row_count
        step_col = step % col_count
        step_local_col = step // col_count
        column = lax.dynamic_slice(
            working, (zero, zero, step_local_col, zero), (per_dev, width, 1, width)
        ).reshape(per_dev, width, width)
        row_raw = from_root(column, "gy", step_col)
        whole = lax.all_gather(row_raw, "gx", axis=0, tiled=True).reshape(
            row_count, per_dev, width, width
        )
        own_diag = lax.dynamic_slice(
            whole, (step_row, step_local_row, zero, zero), (1, 1, width, width)
        ).reshape(width, width)
        chol = jnp.linalg.cholesky(own_diag)
        stacked = whole.transpose(3, 0, 1, 2).reshape(width, row_count * per_dev * width)
        solved = jax.scipy.linalg.solve_triangular(chol, stacked, lower=True)
        panel_all = solved.reshape(width, row_count, per_dev, width).transpose(1, 2, 3, 0)
        panel_all = jnp.where((block_ids > step)[:, :, None, None], panel_all, 0.0)
        row_panel = lax.dynamic_index_in_dim(panel_all, row_index, 0, keepdims=False)
        col_panel = lax.dynamic_index_in_dim(panel_all, col_index, 0, keepdims=False)
        working = working - jnp.einsum(
            "rxk,cyk->rxcy", row_panel, col_panel, precision=lax.Precision.HIGHEST
        )
        on_diag = (jnp.arange(per_dev, dtype=jnp.int32) == step_local_row) & (row_index == step_row)
        new_column = row_panel + jnp.where(on_diag[:, None, None], chol[None], 0.0)
        old_column = lax.dynamic_slice(
            factor, (zero, zero, step_local_col, zero), (per_dev, width, 1, width)
        ).reshape(per_dev, width, width)
        kept = jnp.where(col_index == step_col, new_column, old_column)
        factor = lax.dynamic_update_slice(
            factor, kept.reshape(per_dev, width, 1, width), (zero, zero, step_local_col, zero)
        )
        pivots = lax.dynamic_update_slice(pivots, chol[None], (step, zero, zero))
        return (working, factor, pivots)

    start_state = (matrix, jnp.zeros_like(matrix), jnp.zeros((nblock, width, width), jnp.float32))
    _, factor, pivots = lax.fori_loop(0, nblock, factor_step, start_state)
    shaped = factor.reshape(1, per_dev, width, 1, per_dev, width)
    across = lax.all_gather(shaped, "gy", axis=3, tiled=True)
    whole = lax.all_gather(across, "gx", axis=0, tiled=True)
    lower = whole.transpose(1, 0, 2, 4, 3, 5).reshape(nblock * width, nblock * width)
    middle = jax.scipy.linalg.solve_triangular(lower, rhs.reshape(-1), lower=True)
    answer = jax.scipy.linalg.solve_triangular(lower, middle, lower=True, trans=1)
    solution = answer.reshape(nblock, width)
    return (factor.reshape(1, per_dev, width, 1, per_dev, width), solution)


def solution(mesh):
    in_specs = (
        P(("gx", "gy", "gz"), None),
        P(("gx", "gy", "gz"), None, None),
        P(("gx", "gy", "gz")),
    )
    out_specs = (P("gx", None, None, "gy", None, None), P())
    return jax.shard_map(
        on_device, mesh=mesh, in_specs=in_specs, out_specs=out_specs, check_vma=False
    )
```

profile of v0, /device:TPU:0, one launch (start us, length us, event | category | flops | bytes accessed | tf_op | source)
XLA Modules:
  0.0 2390.1 jit_solution(993266467958038092)
XLA Ops:
  12.8 12.5 multiply_bitcast_fusion
  25.3 19.2 copy.45
  44.6 27.7 %reduce-scatter.3.cloned.1.call-done = f32[16,4,64,4,128]{4,2,3,1,0:T(8,128)} async-done(((f32[16,4,128,4,128]{4,2,3,1,0:T(8,128)}), f32[16,4,64,4,128]{4,2,3,1,0:T(8,128)}) %reduce-scatter.3.cloned.1.call-update) | async-done | bytes 8388624 | tf_op jit(solution)/shard_map/reduce_scatter | solution.py:43
  72.6 183.6 %reduce-scatter.5.cloned.1.call-done = f32[1,4,64,4,128]{4,2,3,1,0:T(8,128)} async-done(((f32[16,4,64,4,128]{4,2,3,1,0:T(8,128)}), f32[1,4,64,4,128]{4,2,3,1,0:T(8,128)}) %reduce-scatter.5.cloned.1.call-update) | async-done | bytes 524304 | tf_op jit(solution)/shard_map/reduce_scatter | solution.py:44
  266.5 1563.0 %while.20 = (s32[]{:T(128)}, f32[4,128,4,128]{3,1,2,0:T(8,128)}, f32[4,128,4,128]{3,1,2,0:T(8,128)S(1)}, s32[]{:T(128)}, s32[]{:T(128)}, /*index=5*/s32[]{:T(128...) while((s32[]{:T(128)}, f32[4,128,4,128]{3,1,2,0:T(8,128)}, ...), condition=%wide.region_6.7_spmd.clone, body=%wide.region_2.6_spmd.clone.sunk | while | flops 806305984 | bytes 14485572 | solution.py:92
  268.4 38.3 %all-reduce.2.cloned.1.call-done = f32[4,128,128]{2,1,0:T(8,128)} async-done(((f32[4,128,128]{2,1,0:T(8,128)}), f32[4,128,128]{2,1,0:T(8,128)}) %all-reduce.2.cloned.1.call-update) | async-done | bytes 262160 | tf_op jit(solution)/shard_map/while/body/eval_jaxpr/psum | solution.py:12
  306.9 27.9 %all-gather.12.cloned.1.call-done = f32[16,128,128]{2,1,0:T(8,128)} async-done(((f32[4,128,128]{2,1,0:T(8,128)}), f32[16,128,128]{2,1,0:T(8,128)}) %all-gather.12.cloned.1.call-update) | async-done | bytes 1048592 | tf_op jit(solution)/shard_map/while/body/eval_jaxpr/all_gather | solution.py:63
  336.6 11.7 cholesky.65
  367.0 37.0 %all-reduce.2.cloned.1.call-done = f32[4,128,128]{2,1,0:T(8,128)} async-done(((f32[4,128,128]{2,1,0:T(8,128)}), f32[4,128,128]{2,1,0:T(8,128)}) %all-reduce.2.cloned.1.call-update) | async-done | bytes 262160 | tf_op jit(solution)/shard_map/while/body/eval_jaxpr/psum | solution.py:12
  404.1 28.1 %all-gather.12.cloned.1.call-done = f32[16,128,128]{2,1,0:T(8,128)} async-done(((f32[4,128,128]{2,1,0:T(8,128)}), f32[16,128,128]{2,1,0:T(8,128)}) %all-gather.12.cloned.1.call-update) | async-done | bytes 1048592 | tf_op jit(solution)/shard_map/while/body/eval_jaxpr/all_gather | solution.py:63
  434.0 11.7 cholesky.65
  464.3 37.5 %all-reduce.2.cloned.1.call-done = f32[4,128,128]{2,1,0:T(8,128)} async-done(((f32[4,128,128]{2,1,0:T(8,128)}), f32[4,128,128]{2,1,0:T(8,128)}) %all-reduce.2.cloned.1.call-update) | async-done | bytes 262160 | tf_op jit(solution)/shard_map/while/body/eval_jaxpr/psum | solution.py:12
  502.0 28.1 %all-gather.12.cloned.1.call-done = f32[16,128,128]{2,1,0:T(8,128)} async-done(((f32[4,128,128]{2,1,0:T(8,128)}), f32[16,128,128]{2,1,0:T(8,128)}) %all-gather.12.cloned.1.call-update) | async-done | bytes 1048592 | tf_op jit(solution)/shard_map/while/body/eval_jaxpr/all_gather | solution.py:63
  531.9 11.7 cholesky.65
  562.3 37.2 %all-reduce.2.cloned.1.call-done = f32[4,128,128]{2,1,0:T(8,128)} async-done(((f32[4,128,128]{2,1,0:T(8,128)}), f32[4,128,128]{2,1,0:T(8,128)}) %all-reduce.2.cloned.1.call-update) | async-done | bytes 262160 | tf_op jit(solution)/shard_map/while/body/eval_jaxpr/psum | solution.py:12
  599.6 28.1 %all-gather.12.cloned.1.call-done = f32[16,128,128]{2,1,0:T(8,128)} async-done(((f32[4,128,128]{2,1,0:T(8,128)}), f32[16,128,128]{2,1,0:T(8,128)}) %all-gather.12.cloned.1.call-update) | async-done | bytes 1048592 | tf_op jit(solution)/shard_map/while/body/eval_jaxpr/all_gather | solution.py:63
  659.8 37.2 %all-reduce.2.cloned.1.call-done = f32[4,128,128]{2,1,0:T(8,128)} async-done(((f32[4,128,128]{2,1,0:T(8,128)}), f32[4,128,128]{2,1,0:T(8,128)}) %all-reduce.2.cloned.1.call-update) | async-done | bytes 262160 | tf_op jit(solution)/shard_map/while/body/eval_jaxpr/psum | solution.py:12
  697.2 28.1 %all-gather.12.cloned.1.call-done = f32[16,128,128]{2,1,0:T(8,128)} async-done(((f32[4,128,128]{2,1,0:T(8,128)}), f32[16,128,128]{2,1,0:T(8,128)}) %all-gather.12.cloned.1.call-update) | async-done | bytes 1048592 | tf_op jit(solution)/shard_map/while/body/eval_jaxpr/all_gather | solution.py:63
  757.4 37.2 %all-reduce.2.cloned.1.call-done = f32[4,128,128]{2,1,0:T(8,128)} async-done(((f32[4,128,128]{2,1,0:T(8,128)}), f32[4,128,128]{2,1,0:T(8,128)}) %all-reduce.2.cloned.1.call-update) | async-done | bytes 262160 | tf_op jit(solution)/shard_map/while/body/eval_jaxpr/psum | solution.py:12
  794.8 27.9 %all-gather.12.cloned.1.call-done = f32[16,128,128]{2,1,0:T(8,128)} async-done(((f32[4,128,128]{2,1,0:T(8,128)}), f32[16,128,128]{2,1,0:T(8,128)}) %all-gather.12.cloned.1.call-update) | async-done | bytes 1048592 | tf_op jit(solution)/shard_map/while/body/eval_jaxpr/all_gather | solution.py:63
  854.8 37.2 %all-reduce.2.cloned.1.call-done = f32[4,128,128]{2,1,0:T(8,128)} async-done(((f32[4,128,128]{2,1,0:T(8,128)}), f32[4,128,128]{2,1,0:T(8,128)}) %all-reduce.2.cloned.1.call-update) | async-done | bytes 262160 | tf_op jit(solution)/shard_map/while/body/eval_jaxpr/psum | solution.py:12
  892.2 27.9 %all-gather.12.cloned.1.call-done = f32[16,128,128]{2,1,0:T(8,128)} async-done(((f32[4,128,128]{2,1,0:T(8,128)}), f32[16,128,128]{2,1,0:T(8,128)}) %all-gather.12.cloned.1.call-update) | async-done | bytes 1048592 | tf_op jit(solution)/shard_map/while/body/eval_jaxpr/all_gather | solution.py:63
  952.3 37.2 %all-reduce.2.cloned.1.call-done = f32[4,128,128]{2,1,0:T(8,128)} async-done(((f32[4,128,128]{2,1,0:T(8,128)}), f32[4,128,128]{2,1,0:T(8,128)}) %all-reduce.2.cloned.1.call-update) | async-done | bytes 262160 | tf_op jit(solution)/shard_map/while/body/eval_jaxpr/psum | solution.py:12
  989.6 28.1 %all-gather.12.cloned.1.call-done = f32[16,128,128]{2,1,0:T(8,128)} async-done(((f32[4,128,128]{2,1,0:T(8,128)}), f32[16,128,128]{2,1,0:T(8,128)}) %all-gather.12.cloned.1.call-update) | async-done | bytes 1048592 | tf_op jit(solution)/shard_map/while/body/eval_jaxpr/all_gather | solution.py:63
  1049.8 37.2 %all-reduce.2.cloned.1.call-done = f32[4,128,128]{2,1,0:T(8,128)} async-done(((f32[4,128,128]{2,1,0:T(8,128)}), f32[4,128,128]{2,1,0:T(8,128)}) %all-reduce.2.cloned.1.call-update) | async-done | bytes 262160 | tf_op jit(solution)/shard_map/while/body/eval_jaxpr/psum | solution.py:12
  1087.2 28.1 %all-gather.12.cloned.1.call-done = f32[16,128,128]{2,1,0:T(8,128)} async-done(((f32[4,128,128]{2,1,0:T(8,128)}), f32[16,128,128]{2,1,0:T(8,128)}) %all-gather.12.cloned.1.call-update) | async-done | bytes 1048592 | tf_op jit(solution)/shard_map/while/body/eval_jaxpr/all_gather | solution.py:63
  1147.4 37.5 %all-reduce.2.cloned.1.call-done = f32[4,128,128]{2,1,0:T(8,128)} async-done(((f32[4,128,128]{2,1,0:T(8,128)}), f32[4,128,128]{2,1,0:T(8,128)}) %all-reduce.2.cloned.1.call-update) | async-done | bytes 262160 | tf_op jit(solution)/shard_map/while/body/eval_jaxpr/psum | solution.py:12
  1185.1 28.1 %all-gather.12.cloned.1.call-done = f32[16,128,128]{2,1,0:T(8,128)} async-done(((f32[4,128,128]{2,1,0:T(8,128)}), f32[16,128,128]{2,1,0:T(8,128)}) %all-gather.12.cloned.1.call-update) | async-done | bytes 1048592 | tf_op jit(solution)/shard_map/while/body/eval_jaxpr/all_gather | solution.py:63
  1245.3 37.2 %all-reduce.2.cloned.1.call-done = f32[4,128,128]{2,1,0:T(8,128)} async-done(((f32[4,128,128]{2,1,0:T(8,128)}), f32[4,128,128]{2,1,0:T(8,128)}) %all-reduce.2.cloned.1.call-update) | async-done | bytes 262160 | tf_op jit(solution)/shard_map/while/body/eval_jaxpr/psum | solution.py:12
  1282.7 28.1 %all-gather.12.cloned.1.call-done = f32[16,128,128]{2,1,0:T(8,128)} async-done(((f32[4,128,128]{2,1,0:T(8,128)}), f32[16,128,128]{2,1,0:T(8,128)}) %all-gather.12.cloned.1.call-update) | async-done | bytes 1048592 | tf_op jit(solution)/shard_map/while/body/eval_jaxpr/all_gather | solution.py:63
  1342.9 37.2 %all-reduce.2.cloned.1.call-done = f32[4,128,128]{2,1,0:T(8,128)} async-done(((f32[4,128,128]{2,1,0:T(8,128)}), f32[4,128,128]{2,1,0:T(8,128)}) %all-reduce.2.cloned.1.call-update) | async-done | bytes 262160 | tf_op jit(solution)/shard_map/while/body/eval_jaxpr/psum | solution.py:12
  1380.2 27.9 %all-gather.12.cloned.1.call-done = f32[16,128,128]{2,1,0:T(8,128)} async-done(((f32[4,128,128]{2,1,0:T(8,128)}), f32[16,128,128]{2,1,0:T(8,128)}) %all-gather.12.cloned.1.call-update) | async-done | bytes 1048592 | tf_op jit(solution)/shard_map/while/body/eval_jaxpr/all_gather | solution.py:63
  1440.3 37.5 %all-reduce.2.cloned.1.call-done = f32[4,128,128]{2,1,0:T(8,128)} async-done(((f32[4,128,128]{2,1,0:T(8,128)}), f32[4,128,128]{2,1,0:T(8,128)}) %all-reduce.2.cloned.1.call-update) | async-done | bytes 262160 | tf_op jit(solution)/shard_map/while/body/eval_jaxpr/psum | solution.py:12
  1478.0 28.1 %all-gather.12.cloned.1.call-done = f32[16,128,128]{2,1,0:T(8,128)} async-done(((f32[4,128,128]{2,1,0:T(8,128)}), f32[16,128,128]{2,1,0:T(8,128)}) %all-gather.12.cloned.1.call-update) | async-done | bytes 1048592 | tf_op jit(solution)/shard_map/while/body/eval_jaxpr/all_gather | solution.py:63
  1538.2 37.2 %all-reduce.2.cloned.1.call-done = f32[4,128,128]{2,1,0:T(8,128)} async-done(((f32[4,128,128]{2,1,0:T(8,128)}), f32[4,128,128]{2,1,0:T(8,128)}) %all-reduce.2.cloned.1.call-update) | async-done | bytes 262160 | tf_op jit(solution)/shard_map/while/body/eval_jaxpr/psum | solution.py:12
  1575.6 28.1 %all-gather.12.cloned.1.call-done = f32[16,128,128]{2,1,0:T(8,128)} async-done(((f32[4,128,128]{2,1,0:T(8,128)}), f32[16,128,128]{2,1,0:T(8,128)}) %all-gather.12.cloned.1.call-update) | async-done | bytes 1048592 | tf_op jit(solution)/shard_map/while/body/eval_jaxpr/all_gather | solution.py:63
  1635.8 37.5 %all-reduce.2.cloned.1.call-done = f32[4,128,128]{2,1,0:T(8,128)} async-done(((f32[4,128,128]{2,1,0:T(8,128)}), f32[4,128,128]{2,1,0:T(8,128)}) %all-reduce.2.cloned.1.call-update) | async-done | bytes 262160 | tf_op jit(solution)/shard_map/while/body/eval_jaxpr/psum | solution.py:12
  1673.5 27.9 %all-gather.12.cloned.1.call-done = f32[16,128,128]{2,1,0:T(8,128)} async-done(((f32[4,128,128]{2,1,0:T(8,128)}), f32[16,128,128]{2,1,0:T(8,128)}) %all-gather.12.cloned.1.call-update) | async-done | bytes 1048592 | tf_op jit(solution)/shard_map/while/body/eval_jaxpr/all_gather | solution.py:63
  1733.5 37.5 %all-reduce.2.cloned.1.call-done = f32[4,128,128]{2,1,0:T(8,128)} async-done(((f32[4,128,128]{2,1,0:T(8,128)}), f32[4,128,128]{2,1,0:T(8,128)}) %all-reduce.2.cloned.1.call-update) | async-done | bytes 262160 | tf_op jit(solution)/shard_map/while/body/eval_jaxpr/psum | solution.py:12
  1771.2 28.1 %all-gather.12.cloned.1.call-done = f32[16,128,128]{2,1,0:T(8,128)} async-done(((f32[4,128,128]{2,1,0:T(8,128)}), f32[16,128,128]{2,1,0:T(8,128)}) %all-gather.12.cloned.1.call-update) | async-done | bytes 1048592 | tf_op jit(solution)/shard_map/while/body/eval_jaxpr/all_gather | solution.py:63
  1830.7 81.8 %all-gather.10.cloned.1.call-done = f32[4,128,16,128]{3,1,2,0:T(8,128)} async-done(((f32[4,128,4,128]{3,1,2,0:T(8,128)}), f32[4,128,16,128]{3,1,2,0:T(8,128)}) %all-gather.10.cloned.1.call-update) | async-done | bytes 4194320 | tf_op jit(solution)/shard_map/all_gather | solution.py:94
  1916.3 39.9 %psum.21 = f32[16,128]{1,0:T(8,128)S(1)} all-reduce(f32[16,128]{1,0:T(8,128)S(1)} %fusion.18), channel_id=1, replica_groups=mesh['gx'=4,'gy'=4,'gz'=2] {'gx','gy','gz'}, use_global_device_ids=true, to_apply=%region_7.8 | all-reduce | flops 2048 | bytes 16384 | tf_op jit(solution)/shard_map/psum | solution.py:38
  1959.0 111.7 %all-gather.8.cloned.1.call-done = f32[4,4,128,4,4,128]{5,2,4,3,1,0:T(8,128)} async-done(((f32[1,4,128,4,4,128]{5,2,4,3,1,0:T(8,128)}), f32[4,4,128,4,4,128]{5,2,4,3,1,0:T(8,128)}) %all-gather.8.cloned.1.call-update) | async-done | bytes 16777232 | tf_op jit(solution)/shard_map/all_gather | solution.py:95
  2070.7 20.9 copy.47
  2091.6 19.9 reshape.543
  2111.5 12.4 fusion.10
  2123.9 47.6 %while.19 = (s32[]{:T(128)}, f32[2048,2048]{1,0:T(8,128)}, s32[16,2]{0,1:T(2,128)S(1)}, f32[16,128,128]{2,1,0:T(8,128)S(1)}, s32[]{:T(128)}) while((s32[]{:T(128)}, f32[2048,2048]{1,0:T(8,128)}, s32[16,2]{0,1:T(2,128)S(1)}, f32[16,128,128]{2,1,0:T(8,128)S(1)}, s32[]{:T(128)}) %tuple.184), condition=%wide.while_cond, body=%wide.while_body.sunk | while | flops 2 | bytes 131181 | solution.py:98
  2171.6 157.4 %custom-call.28 = f32[16,128,128]{1,2,0:T(8,128)S(1)} custom-call(f32[16,128,128]{2,1,0:T(8,128)S(1)} %get-tuple-element.183), custom_call_target="InvertDiagBlocksLowerTriangular" | custom-call | tf_op jit(solution)/shard_map/jit(_solve_triangular)/triangular_solve | solution.py:98
  (559 shorter events, 603.8 us)
Async XLA Ops:
  7.2 65.2 %reduce-scatter.3.cloned.1.call-start = ((), (), s32[]{:S(2)}) async-start(), calls=%async_computation.2 | async-start | bytes 25165824 | tf_op jit(solution)/shard_map/reduce_scatter | solution.py:43
  44.5 211.7 %reduce-scatter.5.cloned.1.call-start = ((), (), s32[]{:S(2)}) async-start(), calls=%async_computation.3 | async-start | bytes 8912896 | tf_op jit(solution)/shard_map/reduce_scatter | solution.py:44
  72.4 194.0 %all-gather.6.cloned.1.call-start = ((), (), s32[]{:S(2)}) async-start(), calls=%async_computation.4 | async-start | bytes 1572864 | tf_op jit(solution)/shard_map/all_gather | solution.py:45
  266.5 1646.0 %copy-start.1 = (bf16[1024,4,128]{2,1,0:T(4,128)(2,1)S(1)}, bf16[1024,4,128]{2,1,0:T(4,128)(2,1)}, u32[]{:S(2)}) copy-start(bf16[1024,4,128]{2,1,0:T(4,128)(2,1)} %param.6) | copy-start | bytes 3145732
  266.5 1646.0 %copy-start.3 = (f32[1024]{0:T(1024)S(1)}, f32[1024]{0:T(1024)}, u32[]{:S(2)}) copy-start(f32[1024]{0:T(1024)} %param.7) | copy-start | bytes 12292
  266.5 1648.9 %copy-start.2 = (s32[1024,4]{0,1:T(4,128)S(1)}, s32[1024,4]{0,1:T(4,128)}, u32[]{:S(2)}) copy-start(s32[1024,4]{0,1:T(4,128)} %param.5) | copy-start | bytes 49156
  266.5 40.2 %all-reduce.2.cloned.1.call-start = ((), (), s32[]{:S(2)}) async-start(), calls=%async_computation.7 | async-start | bytes 524288 | tf_op jit(solution)/shard_map/while/body/eval_jaxpr/psum | solution.py:12
  268.4 66.4 %all-gather.12.cloned.1.call-start = ((), (), s32[]{:S(2)}) async-start(), calls=%async_computation.8 | async-start | bytes 1310720 | tf_op jit(solution)/shard_map/while/body/eval_jaxpr/all_gather | solution.py:63
  365.1 38.8 %all-reduce.2.cloned.1.call-start = ((), (), s32[]{:S(2)}) async-start(), calls=%async_computation.7 | async-start | bytes 524288 | tf_op jit(solution)/shard_map/while/body/eval_jaxpr/psum | solution.py:12
  366.9 65.3 %all-gather.12.cloned.1.call-start = ((), (), s32[]{:S(2)}) async-start(), calls=%async_computation.8 | async-start | bytes 1310720 | tf_op jit(solution)/shard_map/while/body/eval_jaxpr/all_gather | solution.py:63
  462.5 39.4 %all-reduce.2.cloned.1.call-start = ((), (), s32[]{:S(2)}) async-start(), calls=%async_computation.7 | async-start | bytes 524288 | tf_op jit(solution)/shard_map/while/body/eval_jaxpr/psum | solution.py:12
  464.3 65.8 %all-gather.12.cloned.1.call-start = ((), (), s32[]{:S(2)}) async-start(), calls=%async_computation.8 | async-start | bytes 1310720 | tf_op jit(solution)/shard_map/while/body/eval_jaxpr/all_gather | solution.py:63
  560.4 39.0 %all-reduce.2.cloned.1.call-start = ((), (), s32[]{:S(2)}) async-start(), calls=%async_computation.7 | async-start | bytes 524288 | tf_op jit(solution)/shard_map/while/body/eval_jaxpr/psum | solution.py:12
  562.2 65.5 %all-gather.12.cloned.1.call-start = ((), (), s32[]{:S(2)}) async-start(), calls=%async_computation.8 | async-start | bytes 1310720 | tf_op jit(solution)/shard_map/while/body/eval_jaxpr/all_gather | solution.py:63
  658.0 39.0 %all-reduce.2.cloned.1.call-start = ((), (), s32[]{:S(2)}) async-start(), calls=%async_computation.7 | async-start | bytes 524288 | tf_op jit(solution)/shard_map/while/body/eval_jaxpr/psum | solution.py:12
  659.8 65.5 %all-gather.12.cloned.1.call-start = ((), (), s32[]{:S(2)}) async-start(), calls=%async_computation.8 | async-start | bytes 1310720 | tf_op jit(solution)/shard_map/while/body/eval_jaxpr/all_gather | solution.py:63
  755.6 39.0 %all-reduce.2.cloned.1.call-start = ((), (), s32[]{:S(2)}) async-start(), calls=%async_computation.7 | async-start | bytes 524288 | tf_op jit(solution)/shard_map/while/body/eval_jaxpr/psum | solution.py:12
  757.4 65.3 %all-gather.12.cloned.1.call-start = ((), (), s32[]{:S(2)}) async-start(), calls=%async_computation.8 | async-start | bytes 1310720 | tf_op jit(solution)/shard_map/while/body/eval_jaxpr/all_gather | solution.py:63
  853.0 39.0 %all-reduce.2.cloned.1.call-start = ((), (), s32[]{:S(2)}) async-start(), calls=%async_computation.7 | async-start | bytes 524288 | tf_op jit(solution)/shard_map/while/body/eval_jaxpr/psum | solution.py:12
  854.8 65.3 %all-gather.12.cloned.1.call-start = ((), (), s32[]{:S(2)}) async-start(), calls=%async_computation.8 | async-start | bytes 1310720 | tf_op jit(solution)/shard_map/while/body/eval_jaxpr/all_gather | solution.py:63
  950.4 39.0 %all-reduce.2.cloned.1.call-start = ((), (), s32[]{:S(2)}) async-start(), calls=%async_computation.7 | async-start | bytes 524288 | tf_op jit(solution)/shard_map/while/body/eval_jaxpr/psum | solution.py:12
  952.2 65.5 %all-gather.12.cloned.1.call-start = ((), (), s32[]{:S(2)}) async-start(), calls=%async_computation.8 | async-start | bytes 1310720 | tf_op jit(solution)/shard_map/while/body/eval_jaxpr/all_gather | solution.py:63
  1048.0 39.0 %all-reduce.2.cloned.1.call-start = ((), (), s32[]{:S(2)}) async-start(), calls=%async_computation.7 | async-start | bytes 524288 | tf_op jit(solution)/shard_map/while/body/eval_jaxpr/psum | solution.py:12
  1049.8 65.5 %all-gather.12.cloned.1.call-start = ((), (), s32[]{:S(2)}) async-start(), calls=%async_computation.8 | async-start | bytes 1310720 | tf_op jit(solution)/shard_map/while/body/eval_jaxpr/all_gather | solution.py:63
  1145.6 39.4 %all-reduce.2.cloned.1.call-start = ((), (), s32[]{:S(2)}) async-start(), calls=%async_computation.7 | async-start | bytes 524288 | tf_op jit(solution)/shard_map/while/body/eval_jaxpr/psum | solution.py:12
  1147.4 65.8 %all-gather.12.cloned.1.call-start = ((), (), s32[]{:S(2)}) async-start(), calls=%async_computation.8 | async-start | bytes 1310720 | tf_op jit(solution)/shard_map/while/body/eval_jaxpr/all_gather | solution.py:63
  1243.5 39.0 %all-reduce.2.cloned.1.call-start = ((), (), s32[]{:S(2)}) async-start(), calls=%async_computation.7 | async-start | bytes 524288 | tf_op jit(solution)/shard_map/while/body/eval_jaxpr/psum | solution.py:12
  1245.3 65.5 %all-gather.12.cloned.1.call-start = ((), (), s32[]{:S(2)}) async-start(), calls=%async_computation.8 | async-start | bytes 1310720 | tf_op jit(solution)/shard_map/while/body/eval_jaxpr/all_gather | solution.py:63
  1341.1 39.0 %all-reduce.2.cloned.1.call-start = ((), (), s32[]{:S(2)}) async-start(), calls=%async_computation.7 | async-start | bytes 524288 | tf_op jit(solution)/shard_map/while/body/eval_jaxpr/psum | solution.py:12
  1342.8 65.3 %all-gather.12.cloned.1.call-start = ((), (), s32[]{:S(2)}) async-start(), calls=%async_computation.8 | async-start | bytes 1310720 | tf_op jit(solution)/shard_map/while/body/eval_jaxpr/all_gather | solution.py:63
  1438.5 39.4 %all-reduce.2.cloned.1.call-start = ((), (), s32[]{:S(2)}) async-start(), calls=%async_computation.7 | async-start | bytes 524288 | tf_op jit(solution)/shard_map/while/body/eval_jaxpr/psum | solution.py:12
  1440.3 65.8 %all-gather.12.cloned.1.call-start = ((), (), s32[]{:S(2)}) async-start(), calls=%async_computation.8 | async-start | bytes 1310720 | tf_op jit(solution)/shard_map/while/body/eval_jaxpr/all_gather | solution.py:63
  1536.4 39.0 %all-reduce.2.cloned.1.call-start = ((), (), s32[]{:S(2)}) async-start(), calls=%async_computation.7 | async-start | bytes 524288 | tf_op jit(solution)/shard_map/while/body/eval_jaxpr/psum | solution.py:12
  1538.2 65.5 %all-gather.12.cloned.1.call-start = ((), (), s32[]{:S(2)}) async-start(), calls=%async_computation.8 | async-start | bytes 1310720 | tf_op jit(solution)/shard_map/while/body/eval_jaxpr/all_gather | solution.py:63
  1634.0 39.3 %all-reduce.2.cloned.1.call-start = ((), (), s32[]{:S(2)}) async-start(), calls=%async_computation.7 | async-start | bytes 524288 | tf_op jit(solution)/shard_map/while/body/eval_jaxpr/psum | solution.py:12
  1635.7 65.7 %all-gather.12.cloned.1.call-start = ((), (), s32[]{:S(2)}) async-start(), calls=%async_computation.8 | async-start | bytes 1310720 | tf_op jit(solution)/shard_map/while/body/eval_jaxpr/all_gather | solution.py:63
  1731.7 39.3 %all-reduce.2.cloned.1.call-start = ((), (), s32[]{:S(2)}) async-start(), calls=%async_computation.7 | async-start | bytes 524288 | tf_op jit(solution)/shard_map/while/body/eval_jaxpr/psum | solution.py:12
  1733.5 65.8 %all-gather.12.cloned.1.call-start = ((), (), s32[]{:S(2)}) async-start(), calls=%async_computation.8 | async-start | bytes 1310720 | tf_op jit(solution)/shard_map/while/body/eval_jaxpr/all_gather | solution.py:63
  1829.6 1.0 copy-start
  1829.6 82.8 %all-gather.10.cloned.1.call-start = ((), (), s32[]{:S(2)}) async-start(), calls=%async_computation.6 | async-start | bytes 5242880 | tf_op jit(solution)/shard_map/all_gather | solution.py:94
  1830.6 240.1 %all-gather.8.cloned.1.call-start = ((), (), s32[]{:S(2)}) async-start(), calls=%async_computation.5 | async-start | bytes 20971520 | tf_op jit(solution)/shard_map/all_gather | solution.py:95
  2382.2 0.6 copy-start.4
Sparse Core Ops, SparseCore 0:
  44.7 27.6 reduce-scatter.2
  74.6 181.5 reduce-scatter.4
  257.8 8.5 all-gather.5
  270.0 36.7 all-reduce.1
  308.4 26.3 all-gather.11
  368.5 35.3 all-reduce.1
  405.8 26.3 all-gather.11
  466.2 35.5 all-reduce.1
  503.7 26.3 all-gather.11
  563.8 35.5 all-reduce.1
  601.3 26.3 all-gather.11
  661.4 35.5 all-reduce.1
  698.9 26.3 all-gather.11
  759.0 35.5 all-reduce.1
  796.3 26.3 all-gather.11
  856.4 35.5 all-reduce.1
  893.7 26.3 all-gather.11
  953.8 35.5 all-reduce.1
  991.3 26.3 all-gather.11
  1051.4 35.5 all-reduce.1
  1088.9 26.3 all-gather.11
  1149.3 35.5 all-reduce.1
  1186.8 26.3 all-gather.11
  1246.9 35.5 all-reduce.1
  1284.4 26.3 all-gather.11
  1344.5 35.5 all-reduce.1
  1381.8 26.3 all-gather.11
  1442.2 35.5 all-reduce.1
  1479.7 26.3 all-gather.11
  1539.8 35.5 all-reduce.1
  1577.3 26.3 all-gather.11
  1637.7 35.5 all-reduce.1
  1675.0 26.3 all-gather.11
  1735.4 35.5 all-reduce.1
  1772.9 26.3 all-gather.11
  1831.7 80.7 all-gather.9
  1914.1 156.5 all-gather.7
where the time goes:
time: 2400 us; the launch traced here: 2390 us
  waiting for transfers between devices  1460 us (61%)
  other arithmetic  584 us (24%)
  matrix products  154 us (6%)
  local copies, waits for them, and re-layouts  131 us (5%)
  blocking collectives  39.9 us (2%)
    psum x16, waiting for transfers between devices, from_root(): return lax.psum(block, axis)  598 us
    all_gather x16, waiting for transfers between devices, factor_step(): lax.all_gather(row_raw, 'gx', axis=0, tiled=True)  449 us
    another operation x48, other arithmetic, factor_step(): chol = jnp.linalg.cholesky(own_diag)  199 us
    reduce_scatter x1, waiting for transfers between devices, on_device(): lax.psum_scatter(halves, ('gx', 'gy'), scatter_dimension=0, tiled=True)  184 us
    another operation x3, other arithmetic, on_device(): jax.scipy.linalg.solve_triangular(lower, middle, lower=True, trans=1)  170 us
    another operation x32, other arithmetic, factor_step(): solved = jax.scipy.linalg.solve_triangular(chol, stacked, lower=True)  168 us
    all_gather x1, waiting for transfers between devices, on_device(): whole = lax.all_gather(across, 'gx', axis=0, tiled=True)  112 us
    all_gather x1, waiting for transfers between devices, on_device(): across = lax.all_gather(shaped, 'gy', axis=3, tiled=True)  81.8 us
  transfers between devices with their start and end apart: 37, of which 37 were waited for; matrix products, arithmetic and copies ran while one was open for 0% of the time, Pallas kernels for 0%

commit v1 on v0

v1 whole, which is shorter than its diff:
```python
import functools

import jax
import jax.numpy as jnp
from jax import lax
from jax.experimental import pallas as pl
from jax.experimental.pallas import tpu as pltpu
from jax.sharding import PartitionSpec as P

G = 2048
BS = 128
SB = 2 * BS
SUB = 8
VMEM_LIMIT = 60 * 1024 * 1024


def mm(a, b, ca, cb, precision=lax.Precision.HIGHEST):
    return lax.dot_general(
        a, b, (((ca,), (cb,)), ((), ())), precision=precision, preferred_element_type=jnp.float32
    )


def panel_start(nblock, k):
    return BS * (nblock * k - (k * (k - 1)) // 2)


def gram_kernel(nblock, scale, blocks_ref, coef_ref, res_ref, out_ref, design):
    slots = coef_ref.shape[0]
    rows = coef_ref.shape[1]
    chunk = 128
    nsuper = nblock // 2

    @pl.loop(0, rows // chunk)
    def _(t):
        at = pl.ds(pl.multiple_of(t * chunk, chunk), chunk)
        idx = blocks_ref[at, :]
        labels = [jnp.broadcast_to(idx[:, s : s + 1], (chunk, BS)) for s in range(slots)]
        values = [coef_ref[s, at, :].astype(jnp.float32) for s in range(slots)]
        for b in range(nblock):
            total = jnp.where(labels[0] == b, values[0], 0.0)
            for s in range(1, slots):
                total = jnp.where(labels[s] == b, values[s], total)
            design[at, b * BS : (b + 1) * BS] = total.astype(jnp.bfloat16)

    res = res_ref[...]
    high = res.astype(jnp.bfloat16)
    rest = res - high.astype(jnp.float32)
    mid = rest.astype(jnp.bfloat16)
    low = (rest - mid.astype(jnp.float32)).astype(jnp.bfloat16)
    row = lax.broadcasted_iota(jnp.int32, (16, rows), 0)
    parts = jnp.where(
        row == 0,
        high.astype(jnp.float32),
        jnp.where(
            row == 1,
            mid.astype(jnp.float32),
            jnp.where(row == 2, low.astype(jnp.float32), 0.0),
        ),
    ).astype(jnp.bfloat16)
    base = panel_start(nblock, nblock)
    out_ref[base:, :] = jnp.zeros((out_ref.shape[0] - base, BS), jnp.float32)
    for b in range(nblock):
        part = mm(parts, design[:, b * BS : (b + 1) * BS], 1, 0, None)
        out_ref[base + b : base + b + 1, :] = jnp.sum(part, axis=0, keepdims=True) * scale

    @pl.loop(0, nsuper)
    def _(jj):
        right = design[:, pl.ds(pl.multiple_of(jj * SB, SB), SB)]
        first = pl.multiple_of(panel_start(nblock, 2 * jj), BS)
        second = pl.multiple_of(panel_start(nblock, 2 * jj + 1), BS)
        block = mm(right, right, 0, 0, None) * scale
        out_ref[pl.ds(first, SB), :] = block[:, :BS]
        out_ref[pl.ds(second, BS), :] = block[BS:, BS:]

        @pl.loop(jj + 1, nsuper)
        def _(ii):
            left = design[:, pl.ds(pl.multiple_of(ii * SB, SB), SB)]
            block = mm(left, right, 0, 0, None) * scale
            down = (ii - jj) * SB
            out_ref[pl.ds(pl.multiple_of(first + down, BS), SB), :] = block[:, :BS]
            out_ref[pl.ds(pl.multiple_of(second + down - BS, BS), SB), :] = block[:, BS:]


def factor_diag(a, e):
    sub = lax.broadcasted_iota(jnp.int32, (SUB, BS), 0)
    shape = (SUB, BS)
    count = BS // SUB

    def lane(x, j):
        return jnp.broadcast_to(x[:, j : j + 1], shape)

    def sublane(x, j):
        return jnp.broadcast_to(x[j : j + 1, :], shape)

    for p in range(count):
        base = p * SUB
        block = a[base : base + SUB, :]
        eblock = e[base : base + SUB, :]
        cols = [lane(block, base + j) for j in range(SUB)]
        scales, rows, erows, upper = [], [], [], {}
        for j in range(SUB):
            inv = lax.rsqrt(sublane(cols[j], j))
            scales.append(inv)
            mult = jnp.where(sub > j, cols[j] * inv, 0.0)
            for k in range(j + 1, SUB):
                upper[j, k] = sublane(cols[k], j) * inv
                cols[k] = cols[k] - mult * upper[j, k]
            row = sublane(block, j) * inv
            erow = sublane(eblock, j) * inv
            block = jnp.where(sub == j, row, block - mult * row)
            eblock = jnp.where(sub == j, erow, eblock - mult * erow)
            rows.append(row)
            erows.append(erow)
        a[base : base + SUB, :] = block
        e[base : base + SUB, :] = eblock
        for i in range(p + 1, count):
            at = slice(i * SUB, (i + 1) * SUB)
            below = a[at, :]
            ebelow = e[at, :]
            cols = [lane(below, base + j) for j in range(SUB)]
            for j in range(SUB):
                mult = cols[j] * scales[j]
                for k in range(j + 1, SUB):
                    cols[k] = cols[k] - mult * upper[j, k]
                below = below - mult * rows[j]
                ebelow = ebelow - mult * erows[j]
            a[at, :] = below
            e[at, :] = ebelow


def factor_kernel(nblock, place_ref, packed_ref, factor_ref, z_ref, w, inverse, a, e, y, sems):
    nsuper = nblock // 2
    size = nblock * BS
    base = panel_start(nblock, nblock)
    copies = []
    for k in range(nblock):
        begin = panel_start(nblock, k)
        copies.append(
            pltpu.make_async_copy(
                packed_ref.at[begin : begin + size - k * BS, :],
                w.at[k, k * BS : size, :],
                sems.at[k],
            )
        )
    copies.append(
        pltpu.make_async_copy(packed_ref.at[base : base + nblock, :], z_ref, sems.at[nblock])
    )
    for copy in copies:
        copy.start()
    for copy in copies:
        copy.wait()
    y[...] = jnp.zeros_like(y)
    for b in range(nblock):
        y[b // 2, 0:1, (b % 2) * BS : (b % 2 + 1) * BS] = z_ref[b : b + 1, :]
    row = lax.broadcasted_iota(jnp.int32, (BS, BS), 0)
    col = lax.broadcasted_iota(jnp.int32, (BS, BS), 1)
    eye = jnp.where(row == col, 1.0, 0.0).astype(jnp.float32)

    def wide(k, start, height):
        at = pl.ds(pl.multiple_of(start, BS), height)
        return jnp.concatenate([w[2 * k, at, :], w[2 * k + 1, at, :]], axis=1)

    @pl.loop(0, nsuper)
    def _(kk):
        top = pl.ds(pl.multiple_of(kk * SB, BS), BS)
        low = pl.ds(pl.multiple_of(kk * SB + BS, BS), BS)
        k = 2 * kk
        l21 = None
        e1 = None
        for half in range(2):
            if half == 0:
                a[...] = w[k, top, :]
            else:
                l21 = mm(w[k, low, :], e1, 1, 1)
                w[k, low, :] = l21
                a[...] = w[k + 1, low, :] - mm(l21, l21, 1, 1)
            e[...] = eye
            factor_diag(a, e)
            chol = jnp.where(row <= col, a[...], 0.0).T
            if half == 0:
                w[k, top, :] = chol
                e1 = jnp.where(row >= col, e[...], 0.0)
                inverse[kk, 0:BS, 0:BS] = e1
                inverse[kk, 0:BS, BS:SB] = jnp.zeros((BS, BS), jnp.float32)
            else:
                w[k + 1, low, :] = chol
                e2 = jnp.where(row >= col, e[...], 0.0)
                inverse[kk, BS:SB, BS:SB] = e2
                inverse[kk, BS:SB, 0:BS] = -mm(e2, mm(l21, e1, 1, 0), 1, 0)
        y[kk] = mm(y[kk], inverse[kk], 1, 1)

        @pl.loop(kk + 1, nsuper)
        def _(ii):
            at = pl.ds(pl.multiple_of(ii * SB, BS), SB)
            panel = mm(wide(kk, ii * SB, SB), inverse[kk], 1, 1)
            w[k, at, :] = panel[:, :BS]
            w[k + 1, at, :] = panel[:, BS:]

        @pl.loop(kk + 1, nsuper)
        def _(jj):
            right = wide(kk, jj * SB, SB)
            y[jj] = y[jj] - mm(y[kk], right, 1, 1)

            @pl.loop(jj, nsuper)
            def _(ii):
                at = pl.ds(pl.multiple_of(ii * SB, BS), SB)
                update = mm(wide(kk, ii * SB, SB), right, 1, 1)
                w[2 * jj, at, :] = w[2 * jj, at, :] - update[:, :BS]
                w[2 * jj + 1, at, :] = w[2 * jj + 1, at, :] - update[:, BS:]

    @pl.loop(0, nsuper)
    def _(step):
        kk = nsuper - 1 - step

        def body(ii, total):
            return total - mm(y[ii], wide(kk, ii * SB, SB), 1, 0)

        total = lax.fori_loop(kk + 1, nsuper, body, y[kk])
        y[kk] = mm(total, inverse[kk], 1, 0)

    for b in range(nblock):
        z_ref[b : b + 1, :] = y[b // 2, 0:1, (b % 2) * BS : (b % 2 + 1) * BS]

    per_row, per_col = factor_ref.shape[0], factor_ref.shape[2] // BS
    rows_of, cols_of = nblock // per_row, nblock // per_col
    for r in range(per_row):
        for c in range(per_col):
            rb = r * rows_of + place_ref[0]
            cb = c * cols_of + place_ref[1]
            block = w[cb, pl.ds(pl.multiple_of(rb * BS, BS), BS), :]
            keep = row + rb * BS >= col + cb * BS
            factor_ref[r, :, c * BS : (c + 1) * BS] = jnp.where(keep, block, 0.0)


def on_device(blocks, coefficients, residuals):
    row_count = lax.axis_size("gx")
    col_count = lax.axis_size("gy")
    axes = ("gx", "gy", "gz")
    devices = row_count * col_count * lax.axis_size("gz")
    rows, slots, width = coefficients.shape
    scale = 1.0 / (rows * devices)
    nblock = G // width
    nsuper = nblock // 2
    used = panel_start(nblock, nblock) + nblock
    total = -(-used // (SUB * devices)) * SUB * devices
    vmem = pl.BlockSpec(memory_space=pltpu.VMEM)
    term = pl.pallas_call(
        functools.partial(gram_kernel, nblock, scale),
        out_shape=jax.ShapeDtypeStruct((total, width), jnp.float32),
        in_specs=[vmem] * 3,
        out_specs=vmem,
        scratch_shapes=[pltpu.VMEM((rows, G), jnp.bfloat16)],
        compiler_params=pltpu.CompilerParams(vmem_limit_bytes=VMEM_LIMIT),
    )(blocks, coefficients.transpose(1, 0, 2), residuals.reshape(1, rows))
    part = lax.psum_scatter(term, axes, scatter_dimension=0, tiled=True)
    packed = lax.all_gather(part, axes, axis=0, tiled=True)
    place = jnp.stack([lax.axis_index("gx"), lax.axis_index("gy")]).astype(jnp.int32)
    per_row, per_col = nblock // row_count, nblock // col_count
    factor, answer = pl.pallas_call(
        functools.partial(factor_kernel, nblock),
        out_shape=(
            jax.ShapeDtypeStruct((per_row, width, per_col * width), jnp.float32),
            jax.ShapeDtypeStruct((nblock, width), jnp.float32),
        ),
        in_specs=[pl.BlockSpec(memory_space=pltpu.SMEM), pl.BlockSpec(memory_space=pl.ANY)],
        out_specs=(vmem, vmem),
        scratch_shapes=[
            pltpu.VMEM((nblock, G, width), jnp.float32),
            pltpu.VMEM((nsuper, SB, SB), jnp.float32),
            pltpu.VMEM((width, width), jnp.float32),
            pltpu.VMEM((width, width), jnp.float32),
            pltpu.VMEM((nsuper, SUB, SB), jnp.float32),
            pltpu.SemaphoreType.DMA((nblock + 1,)),
        ],
        compiler_params=pltpu.CompilerParams(vmem_limit_bytes=VMEM_LIMIT),
    )(place, packed)
    return (factor.reshape(1, per_row, width, 1, per_col, width), answer)


def solution(mesh):
    in_specs = (
        P(("gx", "gy", "gz"), None),
        P(("gx", "gy", "gz"), None, None),
        P(("gx", "gy", "gz")),
    )
    out_specs = (P("gx", None, None, "gy", None, None), P())
    return jax.shard_map(
        on_device, mesh=mesh, in_specs=in_specs, out_specs=out_specs, check_vma=False
    )
```

time: 2400 us -> 407 us (0.17)
  waiting for transfers between devices: 1460 us -> 219 us
  other arithmetic: 584 us -> 0.65 us
  Pallas kernels: 0 us -> 167 us
  matrix products: 154 us -> 0 us
  local copies, waits for them, and re-layouts: 131 us -> 6.64 us
  blocking collectives: 39.9 us -> 0 us
    psum x16 -> x0, waiting for transfers between devices: 598 us -> none  [from_root(): return lax.psum(block, axis)]
    all_gather x19 -> x1, waiting for transfers between devices: 652 us -> 81.2 us  [on_device(): packed = lax.all_gather(part, axes, axis=0, tiled=True)]
    another operation x83 -> x1, other arithmetic: 537 us -> 0.65 us  [on_device(): jnp.stack([lax.axis_index('gx'), lax.axis_index('gy')]).astype(jnp.int32)]
    reduce_scatter x2 -> x0, waiting for transfers between devices: 211 us -> none  [the longest x1 184 us: on_device(): lax.psum_scatter(halves, ('gx', 'gy'), scatter_dimension=0, tiled=True)]
    pallas_call x0 -> x2, Pallas kernels: none -> 167 us  [the longest x1 144 us: on_device(): pl.pallas_call(functools.partial(factor_kernel, nblock), out_shape=(jax.S...]
    unnamed x5 -> x3, waiting for transfers between devices: 0.08 us -> 137 us
    another operation x78 -> x0, matrix products: 86.4 us -> none  [the longest x16 35.1 us: factor_step(): solved = jax.scipy.linalg.solve_triangular(chol, stacked, lower=True)]
    dot_general x19 -> x0, matrix products: 68.1 us -> none  [the longest x16 51.1 us: factor_step(): jnp.einsum('rxk,cyk->rxcy', row_panel, col_panel, precision=lax.Precision...]
  transfers between devices with their start and end apart: 37 -> 2, of which waited for: 37 -> 2; matrix products, arithmetic and copies ran while one was open for 0% -> 0% of each run, Pallas kernels for 0% -> 0%
where the time goes in v1:
time: 407 us
  waiting for transfers between devices  219 us (54%)
  Pallas kernels  167 us (41%)
  between operations  14.1 us (3%)
  local copies, waits for them, and re-layouts  6.64 us (2%)
    pallas_call x1, Pallas kernels, on_device(): pl.pallas_call(functools.partial(factor_kernel, nblock), out_shape=(jax.S...  144 us
    unnamed x3, waiting for transfers between devices  137 us
    all_gather x1, waiting for transfers between devices, on_device(): packed = lax.all_gather(part, axes, axis=0, tiled=True)  81.2 us
    pallas_call x1, Pallas kernels, on_device(): pl.pallas_call(functools.partial(gram_kernel, nblock, scale), out_shape=j...  23.2 us
  transfers between devices with their start and end apart: 2, of which 2 were waited for; matrix products, arithmetic and copies ran while one was open for 0% of the time, Pallas kernels for 0%

profile of v1, /device:TPU:0, one launch (start us, length us, event | category | flops | bytes accessed | tf_op | source)
XLA Modules:
  0.0 407.0 jit_solution(11094567443653476770)
XLA Ops:
  7.2 0.0 reduce-scatter.4.cloned.1.call-start
  7.2 1.8 copy.9.blocks_ref
  9.0 2.3 copy.12
  11.3 23.2 %shard_map.50 = f32[17664,128]{1,0:T(8,128)} custom-call(s32[1024,4]{1,0:T(8,128)} %copy.9.blocks_ref, bf16[4,1024,128]{2,1,0:T(8,128)(2,1)} %bitcast.7, f32[1,1024]{1,0:T(1,128)} %bitcast.9), custom_call_target="tpu_custom_call" | custom-call | tf_op jit(solution)/shard_map/pallas_call | solution.py:247
  34.5 0.0 reduce-scatter.4.cloned.1.call-update
  34.5 0.0 all-gather.2.cloned.1.call-start
  34.6 137.3 %reduce-scatter.4.cloned.1.call-done = f32[552,128]{1,0:T(8,128)} async-done(((f32[17664,128]{1,0:T(8,128)}), f32[552,128]{1,0:T(8,128)}) %reduce-scatter.4.cloned.1.call-update) | async-done | bytes 282640
  171.9 0.0 all-gather.2.cloned.1.call-update
  171.9 0.6 pad_add_fusion.place_ref
  172.6 81.2 %all-gather.2.cloned.1.call-done.packed_ref = f32[17664,128]{1,0:T(8,128)} async-done(((f32[552,128]{1,0:T(8,128)}), f32[17664,128]{1,0:T(8,128)}) %all-gather.2.cloned.1.call-update) | async-done | bytes 9043984 | tf_op jit(solution)/shard_map/all_gather | solution.py:256
  253.7 143.9 %shard_map.51 = (f32[4,128,512]{2,1,0:T(8,128)}, f32[16,128]{1,0:T(8,128)}) custom-call(s32[2]{0:T(128)} %pad_add_fusion.place_ref, f32[17664,128]{1,0:T(8,128)} %all-gather.2.cloned.1.call-done.packed_ref), custom_call_target="tpu_custom_call" | custom-call | tf_op jit(solution)/shard_map/pallas_call | solution.py:259
  397.6 2.5 reshape.11
Async XLA Ops:
  7.2 164.7 %reduce-scatter.4.cloned.1.call-start = ((), (), s32[]{:S(2)}) async-start(), calls=%async_computation.2 | async-start | bytes 9326592
  34.5 219.2 %all-gather.2.cloned.1.call-start = ((), (), s32[]{:S(2)}) async-start(), calls=%async_computation.1 | async-start | bytes 9326592 | tf_op jit(solution)/shard_map/all_gather | solution.py:256
Sparse Core Ops, SparseCore 0:
  34.6 137.2 reduce-scatter.3
  174.9 78.7 all-gather.1

commit v2 on v1

--- a/solution.py
+++ b/solution.py
@@ -18,6 +18,16 @@
     return lax.dot_general(
         a, b, (((ca,), (cb,)), ((), ())), precision=precision, preferred_element_type=jnp.float32
     )
+
+
+def split(x):
+    high = x.astype(jnp.bfloat16)
+    return high, (x - high.astype(jnp.float32)).astype(jnp.bfloat16)
+
+
+def mm3(a, b, ca, cb):
+    (ah, al), (bh, bl) = split(a), b if isinstance(b, tuple) else split(b)
+    return mm(ah, bh, ca, cb, None) + (mm(ah, bl, ca, cb, None) + mm(al, bh, ca, cb, None))
 
 
 def panel_start(nblock, k):
@@ -192,19 +202,19 @@
         @pl.loop(kk + 1, nsuper)
         def _(ii):
             at = pl.ds(pl.multiple_of(ii * SB, BS), SB)
-            panel = mm(wide(kk, ii * SB, SB), inverse[kk], 1, 1)
+            panel = mm3(wide(kk, ii * SB, SB), inverse[kk], 1, 1)
             w[k, at, :] = panel[:, :BS]
             w[k + 1, at, :] = panel[:, BS:]
 
         @pl.loop(kk + 1, nsuper)
         def _(jj):
-            right = wide(kk, jj * SB, SB)
-            y[jj] = y[jj] - mm(y[kk], right, 1, 1)
+            right = split(wide(kk, jj * SB, SB))
+            y[jj] = y[jj] - mm3(y[kk], right, 1, 1)
 
             @pl.loop(jj, nsuper)
             def _(ii):
                 at = pl.ds(pl.multiple_of(ii * SB, BS), SB)
-                update = mm(wide(kk, ii * SB, SB), right, 1, 1)
+                update = mm3(wide(kk, ii * SB, SB), right, 1, 1)
                 w[2 * jj, at, :] = w[2 * jj, at, :] - update[:, :BS]
                 w[2 * jj + 1, at, :] = w[2 * jj + 1, at, :] - update[:, BS:]
 
@@ -213,7 +223,7 @@
         kk = nsuper - 1 - step
 
         def body(ii, total):
-            return total - mm(y[ii], wide(kk, ii * SB, SB), 1, 0)
+            return total - mm3(y[ii], wide(kk, ii * SB, SB), 1, 0)
 
         total = lax.fori_loop(kk + 1, nsuper, body, y[kk])
         y[kk] = mm(total, inverse[kk], 1, 0)
@@ -232,10 +242,192 @@
             factor_ref[r, :, c * BS : (c + 1) * BS] = jnp.where(keep, block, 0.0)
 
 
+def exchange_kernel(nx, ny, n_gz, term_ref, out_ref, halves, stage, slots, s1, r1, s2, r2, s3, r3, s4, r4):
+    n = nx * ny
+    mp, mq = lax.axis_index("gx"), lax.axis_index("gy")
+    me = mp * ny + mq
+    g = lax.axis_index("gz")
+
+    def remote(src, dst, send, recv, device):
+        return pltpu.make_async_remote_copy(
+            src_ref=src,
+            dst_ref=dst,
+            send_sem=send,
+            recv_sem=recv,
+            device_id=device,
+            device_id_type=pl.DeviceIdType.MESH,
+        )
+
+    def half(c, d):
+        peer = lax.rem(g + d, n_gz)
+        return remote(
+            term_ref.at[c, peer],
+            halves.at[d - 1, c],
+            s1.at[d - 1, c],
+            r1.at[d - 1, c],
+            {"gz": peer},
+        )
+
+    def to_row(p, q, slot):
+        at, to = p * ny + q, slot * ny + q
+        return remote(stage.at[at], slots.at[to], s2.at[at], r2.at[to], {"gx": p})
+
+    def to_owner(q, slot):
+        at, to = mp * ny + q, mp * ny + slot
+        return remote(stage.at[at], slots.at[to], s2.at[at], r2.at[to], {"gy": q})
+
+    def out_cols(q, owner):
+        at = mp * ny + owner
+        block = out_ref.at[at, g]
+        return remote(block, block, s3.at[mp * ny + q], r3.at[at], {"gy": q})
+
+    def out_rows(p, q, owner):
+        at = owner * ny + q
+        block = out_ref.at[at, g]
+        return remote(block, block, s3.at[p * ny + q], r3.at[at], {"gx": p})
+
+    def across(c, d, layer):
+        block = out_ref.at[c, layer]
+        return remote(
+            block, block, s4.at[d - 1, c], r4.at[d - 1, c], {"gz": lax.rem(g + d, n_gz)}
+        )
+
+    def combine(c):
+        total = term_ref[c, g]
+        for d in range(1, n_gz):
+            half(c, d).wait_recv()
+            total = total + halves[d - 1, c]
+        return total
+
+    @pl.loop(0, n)
+    def _(i):
+        q = lax.rem(mq + 1 + i // nx, ny)
+        p = lax.rem(mp + 1 + i % nx, nx)
+        for d in range(1, n_gz):
+            half(p * ny + q, d).start()
+
+    @pl.loop(0, ny)
+    def _(i):
+        q = lax.rem(mq + 1 + i, ny)
+
+        @pl.loop(0, nx - 1)
+        def _(j):
+            p = lax.rem(mp + 1 + j, nx)
+            stage[p * ny + q] = combine(p * ny + q)
+            to_row(p, q, mp).start()
+
+    def row_sum(q):
+        at = mp * ny + q
+        stage[at] = combine(at)
+
+        @pl.loop(0, nx - 1)
+        def _(j):
+            p = lax.rem(mp + nx - 1 - j, nx)
+            to_row(p, q, p).wait_recv()
+            stage[at] = stage[at] + slots[p * ny + q]
+
+    @pl.loop(0, ny - 1)
+    def _(i):
+        q = lax.rem(mq + 1 + i, ny)
+        row_sum(q)
+        to_owner(q, mq).start()
+
+    row_sum(mq)
+    out_ref[me, g] = stage[me]
+
+    @pl.loop(0, ny - 1)
+    def _(i):
+        q = lax.rem(mq + ny - 1 - i, ny)
+        to_owner(q, q).wait_recv()
+        out_ref[me, g] = out_ref[me, g] + slots[mp * ny + q]
+
+    def spread(q):
+        @pl.loop(0, nx - 1)
+        def _(j):
+            out_rows(lax.rem(mp + 1 + j, nx), q, mp).start()
+
+        for d in range(1, n_gz):
+            across(mp * ny + q, d, g).start()
+
+    @pl.loop(0, ny - 1)
+    def _(i):
+        out_cols(lax.rem(mq + 1 + i, ny), mq).start()
+
+    spread(mq)
+
+    @pl.loop(0, ny - 1)
+    def _(i):
+        q = lax.rem(mq + ny - 1 - i, ny)
+        out_cols(q, q).wait_recv()
+        spread(q)
+
+    @pl.loop(0, ny)
+    def _(i):
+        q = lax.rem(mq + ny - i, ny)
+
+        @pl.loop(0, nx - 1)
+        def _(j):
+            p = lax.rem(mp + nx - 1 - j, nx)
+            out_rows(p, q, p).wait_recv()
+            for d in range(1, n_gz):
+                across(p * ny + q, d, g).start()
+
+    @pl.loop(0, n)
+    def _(c):
+        for d in range(1, n_gz):
+            across(c, d, lax.rem(g + n_gz - d, n_gz)).wait_recv()
+            across(c, d, g).wait_send()
+            half(c, d).wait_send()
+
+    @pl.loop(0, ny)
+    def _(q):
+        @pl.loop(0, nx - 1)
+        def _(j):
+            p = lax.rem(mp + 1 + j, nx)
+            to_row(p, q, mp).wait_send()
+            out_rows(p, q, mp).wait_send()
+
+    @pl.loop(0, ny - 1)
+    def _(i):
+        q = lax.rem(mq + 1 + i, ny)
+        to_owner(q, mq).wait_send()
+        out_cols(q, mq).wait_send()
+
+
+def exchange(term, row_count, col_count, n_gz):
+    n = row_count * col_count
+    total, width = term.shape
+    part = total // (n * n_gz)
+    shape = (n, n_gz, part, width)
+    vmem = pl.BlockSpec(memory_space=pltpu.VMEM)
+    pair = pltpu.SemaphoreType.DMA((n_gz - 1, n))
+    single = pltpu.SemaphoreType.DMA((n,))
+    out = pl.pallas_call(
+        functools.partial(exchange_kernel, row_count, col_count, n_gz),
+        out_shape=jax.ShapeDtypeStruct(shape, jnp.float32),
+        in_specs=[vmem],
+        out_specs=vmem,
+        scratch_shapes=[
+            pltpu.VMEM((n_gz - 1, n, part, width), jnp.float32),
+            pltpu.VMEM((n, part, width), jnp.float32),
+            pltpu.VMEM((n, part, width), jnp.float32),
+            pair,
+            pair,
+            single,
+            single,
+            single,
+            single,
+            pair,
+            pair,
+        ],
+        compiler_params=pltpu.CompilerParams(vmem_limit_bytes=VMEM_LIMIT, has_side_effects=True),
+    )(term.reshape(shape))
+    return out.reshape(total, width)
+
+
 def on_device(blocks, coefficients, residuals):
     row_count = lax.axis_size("gx")
     col_count = lax.axis_size("gy")
-    axes = ("gx", "gy", "gz")
     devices = row_count * col_count * lax.axis_size("gz")
     rows, slots, width = coefficients.shape
     scale = 1.0 / (rows * devices)
@@ -252,8 +444,7 @@
         scratch_shapes=[pltpu.VMEM((rows, G), jnp.bfloat16)],
         compiler_params=pltpu.CompilerParams(vmem_limit_bytes=VMEM_LIMIT),
     )(blocks, coefficients.transpose(1, 0, 2), residuals.reshape(1, rows))
-    part = lax.psum_scatter(term, axes, scatter_dimension=0, tiled=True)
-    packed = lax.all_gather(part, axes, axis=0, tiled=True)
+    packed = exchange(term, row_count, col_count, lax.axis_size("gz"))
     place = jnp.stack([lax.axis_index("gx"), lax.axis_index("gy")]).astype(jnp.int32)
     per_row, per_col = nblock // row_count, nblock // col_count
     factor, answer = pl.pallas_call(

time: 407 us -> 282 us (0.69)
  waiting for transfers between devices: 219 us -> 0 us
  Pallas kernels: 167 us -> 274 us
  between operations: 14.1 us -> 0.65 us
    unnamed x3 -> x0, waiting for transfers between devices: 137 us -> none
    pallas_call x0 -> x1, Pallas kernels: none -> 121 us  [exchange(): pl.pallas_call(functools.partial(exchange_kernel, row_count, col_count, n...]
    all_gather x1 -> x0, waiting for transfers between devices: 81.2 us -> none  [on_device(): packed = lax.all_gather(part, axes, axis=0, tiled=True)]
    pallas_call x1, Pallas kernels: 144 us -> 130 us  [on_device(): pl.pallas_call(functools.partial(factor_kernel, nblock), out_shape=(jax.S...]
  transfers between devices with their start and end apart: 2 -> 0, of which waited for: 2 -> 0; matrix products, arithmetic and copies ran while one was open for 0% -> 0% of each run, Pallas kernels for 0% -> 0%
where the time goes in v2:
time: 282 us
  Pallas kernels  274 us (97%)
  local copies, waits for them, and re-layouts  6.59 us (2%)
    pallas_call x1, Pallas kernels, on_device(): pl.pallas_call(functools.partial(factor_kernel, nblock), out_shape=(jax.S...  130 us
    pallas_call x1, Pallas kernels, exchange(): pl.pallas_call(functools.partial(exchange_kernel, row_count, col_count, n...  121 us
    pallas_call x1, Pallas kernels, on_device(): pl.pallas_call(functools.partial(gram_kernel, nblock, scale), out_shape=j...  23.2 us

profile of v2, /device:TPU:0, one launch (start us, length us, event | category | flops | bytes accessed | tf_op | source)
XLA Modules:
  0.0 281.8 jit_solution(18175910332414378539)
XLA Ops:
  0.6 0.6 pad_add_fusion.place_ref
  1.3 1.7 copy.6.blocks_ref
  3.0 2.3 copy.9
  5.3 23.2 %shard_map.50 = f32[17664,128]{1,0:T(8,128)} custom-call(s32[1024,4]{1,0:T(8,128)} %copy.6.blocks_ref, bf16[4,1024,128]{2,1,0:T(8,128)(2,1)} %bitcast.11, f32[1,1024]{1,0:T(1,128)} %bitcast.13), custom_call_target="tpu_custom_call" | custom-call | tf_op jit(solution)/shard_map/pallas_call | solution.py:439
  28.5 120.9 %shard_map.51 = f32[16,2,552,128]{3,2,1,0:T(8,128)} custom-call(f32[16,2,552,128]{3,2,1,0:T(8,128)} %bitcast.10), custom_call_target="tpu_custom_call" | custom-call | tf_op jit(solution)/shard_map/pallas_call | solution.py:405
  149.4 129.8 %shard_map.52 = (f32[4,128,512]{2,1,0:T(8,128)}, f32[16,128]{1,0:T(8,128)}) custom-call(s32[2]{0:T(128)} %pad_add_fusion.place_ref, f32[17664,128]{1,0:T(8,128)} %bitcast.9), custom_call_target="tpu_custom_call" | custom-call | tf_op jit(solution)/shard_map/pallas_call | solution.py:450
  279.2 2.5 reshape.19
